TPU v7x, 32 devices: a whole 2x2x4 slice. The times are simulated.
32 devices in a mesh: gx: 2 (over y), gy: 4 (over x, core), gz: 4 (over z).
Axes of the slice: x: 2, y: 2, z: 4, core: 2. Of those that a mesh axis runs over, the one named last changes fastest.
Arguments:
- loads: float32 [16, 4, 16, 1024], P(None, 'gx', 'gy', 'gz'), may hold values from -60 to 60
- moduli: float32 [8], replicated, may hold values from 0.5 to 4
- material: int32 [4, 16, 1024], P('gx', 'gy', 'gz'), may hold values from 0 to 7
Outputs:
- solution: float32 [16, 4, 16, 1024], P(None, 'gx', 'gy', 'gz')
- residual: float32 [16, 4, 16, 1024], P(None, 'gx', 'gy', 'gz')
All inputs are finite; a program needn't handle non-finite values.
Results may differ from a plain program's by a relative error of at most 0.005.
The roundings to bfloat16 on the way count: a program that leaves them out, or rounds other values in their place, can miss the bound.
Values may be sent and summed in bfloat16 or wider, within the bound.
A program may use at most 64 MiB of HBM per device.

v0:
```python
import jax
import jax.numpy as jnp
import numpy as np
from jax import lax
from jax.sharding import PartitionSpec as P

ITERS = 2
SIGMA = 0.25


def padded_2(cells, sides, width):
    for axis, dim in sides:
        count = lax.axis_size(axis)
        ends = count - 1
        head = lax.slice_in_dim(cells, 0, width, axis=dim)
        tail = lax.slice_in_dim(cells, cells.shape[dim] - width, cells.shape[dim], axis=dim)
        cells = jnp.concatenate(
            [
                lax.ppermute(tail, axis, [(i, (i + 1) % count) for i in range(ends)]),
                cells,
                lax.ppermute(head, axis, [((i + 1) % count, i) for i in range(ends)]),
            ],
            axis=dim,
        )
    return cells


def stiffness_table():
    line_mass = np.array([[1.0 / 3.0, 1.0 / 6.0], [1.0 / 6.0, 1.0 / 3.0]])
    line_stiff = np.array([[1.0, -1.0], [-1.0, 1.0]])
    table = np.zeros((8, 8))
    for target in range(8):
        for source in range(8):
            target_bits = [target >> 2 & 1, target >> 1 & 1, target & 1]
            source_bits = [source >> 2 & 1, source >> 1 & 1, source & 1]
            total = 0.0
            for stiff_dim in range(3):
                factor = 1.0
                for other in range(3):
                    if other == stiff_dim:
                        factor = factor * line_stiff[target_bits[other], source_bits[other]]
                    else:
                        factor = factor * line_mass[target_bits[other], source_bits[other]]
                total = total + factor
            table[target, source] = total
    return table


def corner_bits(corner):
    return (corner >> 2 & 1, corner >> 1 & 1, corner & 1)


def apply_operator(field, weights, kernel):
    lowered = field.astype(jnp.bfloat16)
    padded = padded_2(lowered, (("gx", 1), ("gy", 2), ("gz", 3)), 1)
    size_x, size_y, size_z = (field.shape[1], field.shape[2], field.shape[3])
    pieces = []
    for corner in range(8):
        bit_x, bit_y, bit_z = corner_bits(corner)
        pieces.append(
            padded[
                :,
                bit_x : bit_x + size_x + 1,
                bit_y : bit_y + size_y + 1,
                bit_z : bit_z + size_z + 1,
            ]
        )
    stacked = jnp.stack(pieces)
    total = SIGMA * field
    for corner in range(8):
        bit_x, bit_y, bit_z = corner_bits(corner)
        part = (
            jnp.einsum("b,bcxyz->cxyz", kernel[corner], stacked, preferred_element_type=jnp.float32)
            * weights
        )
        total = (
            total
            + part[
                :,
                1 - bit_x : 1 - bit_x + size_x,
                1 - bit_y : 1 - bit_y + size_y,
                1 - bit_z : 1 - bit_z + size_z,
            ]
        )
    return total


def local_gram(left, right):
    return jnp.einsum("cxyz,dxyz->cd", left, right, precision=lax.Precision.HIGHEST)


def combine(block, coeffs):
    return jnp.einsum("cxyz,cd->dxyz", block, coeffs, precision=lax.Precision.HIGHEST)


def solve_small(matrix, rhs_small):
    factor = jnp.linalg.cholesky(matrix)
    return jax.scipy.linalg.cho_solve((factor, True), rhs_small)


def residual_gram(residual):
    return lax.psum(local_gram(residual, residual), ("gx", "gy", "gz"))


def on_device(loads, moduli, material):
    kernel = jnp.asarray(stiffness_table(), jnp.float32).astype(jnp.bfloat16)
    levels = jnp.arange(moduli.shape[0], dtype=jnp.int32)
    node_modulus = jnp.sum(jnp.where(material[..., None] == levels, moduli, 0.0), axis=-1)
    padded_mod = padded_2(node_modulus, (("gx", 0), ("gy", 1), ("gz", 2)), 1)
    size_x, size_y, size_z = material.shape
    weights = jnp.zeros((size_x + 1, size_y + 1, size_z + 1), jnp.float32)
    for corner in range(8):
        bit_x, bit_y, bit_z = corner_bits(corner)
        weights = (
            weights
            + padded_mod[
                bit_x : bit_x + size_x + 1, bit_y : bit_y + size_y + 1, bit_z : bit_z + size_z + 1
            ]
        )
    weights = weights * 0.125
    solution = jnp.zeros_like(loads)
    residual = loads
    direction = loads
    current = residual_gram(residual)
    for iteration in range(ITERS):
        image = apply_operator(direction, weights, kernel)
        curvature, cross, image_sq = lax.psum(
            (local_gram(direction, image), local_gram(image, residual), local_gram(image, image)),
            ("gx", "gy", "gz"),
        )
        alpha = solve_small(curvature, current)
        solution = solution + combine(direction, alpha)
        residual = residual - combine(image, alpha)
        if iteration + 1 < ITERS:
            high = lax.Precision.HIGHEST
            cross_term = jnp.dot(alpha.T, cross, precision=high)
            quad_term = jnp.dot(jnp.dot(alpha.T, image_sq, precision=high), alpha, precision=high)
            updated = current - cross_term - cross_term.T + quad_term
            beta = solve_small(current, updated)
            direction = residual + combine(direction, beta)
            current = updated
    return (solution, residual)


def solution(mesh):
    in_specs = (P(None, "gx", "gy", "gz"), P(), P("gx", "gy", "gz"))
    out_specs = (P(None, "gx", "gy", "gz"), P(None, "gx", "gy", "gz"))
    return jax.shard_map(
        on_device, mesh=mesh, in_specs=in_specs, out_specs=out_specs, check_vma=False
    )
```

profile of v0, /device:TPU:0, one launch (start us, length us, event | category | flops | bytes accessed | tf_op | source)
XLA Modules:
  0.0 185.7 jit_solution(12359744168205889732)
XLA Ops:
  0.6 0.8 select_reduce_fusion
  1.4 4.9 %collective-permute-start.6 = (f32[1,4,256]{2,1,0:T(4,128)S(1)}, f32[1,4,256]{2,1,0:T(4,128)S(1)}, u32[]{:S(2)}, u32[]{:S(2)}) collective-permute-start(f32[1,4,256]{2,1,0:T(4,128)S(1)} %get-tuple-element.42), channel_id=1, source_target_pairs={{0,16},{1,17},{2,18},{3,19},{4,20},{5,21},{6,22},{7,23},{8,24},{9,... | collective-permute-start | bytes 12296 | tf_op jit(solution)/shard_map/ppermute | solution.py:19
  6.4 1.3 collective-permute-start.7
  7.7 0.9 convert_element_type.9
  8.6 4.5 %collective-permute-start = (bf16[16,1,4,256]{3,2,1,0:T(4,128)(2,1)S(1)}, bf16[16,1,4,256]{3,2,1,0:T(4,128)(2,1)S(1)}, u32[]{:S(2)}, u32[]{:S(2)}) collective-permute-start(bf16[16,1,4,256]{3,2,1,0:T(4,128)(2,1)S(1)} %get-tuple-element.26), channel_id=1, source_target_pairs={{0,16},{1,17},{2,18},{3,19},{4,20},{5,21},{6,22},{7,23},{8,24},{9,... | collective-permute-start | bytes 98312 | tf_op jit(solution)/shard_map/ppermute | solution.py:19
  13.2 1.3 collective-permute-start.1
  14.5 1.3 collective-permute-start.8
  15.8 1.3 collective-permute-start.9
  17.1 1.3 convolution_bitcast_fusion.4
  18.4 2.2 %collective-permute-done.9 = f32[4,1,256]{2,1,0:T(1,128)S(1)} collective-permute-done((f32[4,1,256]{2,1,0:T(1,128)S(1)}, f32[4,1,256]{2,1,0:T(1,128)S(1)}, u32[]{:S(2)}, u32[]{:S(2)}) %collective-permute-start.9) | collective-permute-done | bytes 4128 | tf_op jit(solution)/shard_map/ppermute | solution.py:21
  20.7 3.5 %collective-permute-start.10 = (f32[4,6,1]{2,1,0:T(8,128)S(1)}, f32[4,6,1]{2,1,0:T(8,128)S(1)}, u32[]{:S(2)}, u32[]{:S(2)}) collective-permute-start(f32[4,6,1]{2,1,0:T(8,128)S(1)} %get-tuple-element.36), channel_id=1, source_target_pairs={{0,1},{1,2},{2,3},{4,5},{5,6},{6,7},{8,9},{9,10},{10,11},{12,13},{... | collective-permute-start | bytes 296 | tf_op jit(solution)/shard_map/ppermute | solution.py:19
  24.2 1.3 collective-permute-start.11
  25.6 4.2 %collective-permute-done.11 = f32[4,6,1]{2,1,0:T(8,128)S(1)} collective-permute-done((f32[4,6,1]{2,1,0:T(8,128)S(1)}, f32[4,6,1]{2,1,0:T(8,128)S(1)}, u32[]{:S(2)}, u32[]{:S(2)}) %collective-permute-start.11) | collective-permute-done | bytes 128 | tf_op jit(solution)/shard_map/ppermute | solution.py:21
  30.1 2.8 %collective-permute-start.2 = (bf16[16,4,1,256]{3,2,1,0:T(2,128)(2,1)S(1)}, bf16[16,4,1,256]{3,2,1,0:T(2,128)(2,1)S(1)}, u32[]{:S(2)}, u32[]{:S(2)}) collective-permute-start(bf16[16,4,1,256]{3,2,1,0:T(2,128)(2,1)S(1)} %get-tuple-element.22), channel_id=1, source_target_pairs={{0,4},{4,8},{8,12},{1,5},{5,9},{9,13},{2,6},{6,10},{10,14},{3,7},{... | collective-permute-start | bytes 98312 | tf_op jit(solution)/shard_map/ppermute | solution.py:19
  33.0 1.3 collective-permute-start.3
  34.3 2.8 %collective-permute-done.3 = bf16[16,4,1,256]{3,2,1,0:T(2,128)(2,1)S(1)} collective-permute-done((bf16[16,4,1,256]{3,2,1,0:T(2,128)(2,1)S(1)}, bf16[16,4,1,256]{3,2,1,0:T(2,128)(2,1)S(1)}, u32[]{:S(2)}, u32[]{:S(2)}) %collective-permute-start.3) | collective-permute-done | bytes 32800 | tf_op jit(solution)/shard_map/ppermute | solution.py:21
  37.5 3.5 %collective-permute-start.4 = (bf16[16,4,6,1]{3,2,1,0:T(8,128)(2,1)S(1)}, bf16[16,4,6,1]{3,2,1,0:T(8,128)(2,1)S(1)}, u32[]{:S(2)}, u32[]{:S(2)}) collective-permute-start(bf16[16,4,6,1]{3,2,1,0:T(8,128)(2,1)S(1)} %get-tuple-element.15), channel_id=1, source_target_pairs={{0,1},{1,2},{2,3},{4,5},{5,6},{6,7},{8,9},{9,10},{10,11},{12,13},{... | collective-permute-start | bytes 2312 | tf_op jit(solution)/shard_map/ppermute | solution.py:19
  41.0 1.3 collective-permute-start.5
  42.4 1.1 collective-permute-done.4
  43.5 4.4 %collective-permute-done.5 = bf16[16,4,6,1]{3,2,1,0:T(8,128)(2,1)S(1)} collective-permute-done((bf16[16,4,6,1]{3,2,1,0:T(8,128)(2,1)S(1)}, bf16[16,4,6,1]{3,2,1,0:T(8,128)(2,1)S(1)}, u32[]{:S(2)}, u32[]{:S(2)}) %collective-permute-start.5) | collective-permute-done | bytes 800 | tf_op jit(solution)/shard_map/ppermute | solution.py:21
  47.8 0.9 pad_maximum_fusion
  49.3 1.6 copy.46
  51.0 0.5 fusion.82
  51.6 0.5 fusion.83
  52.2 0.5 fusion.84
  52.7 0.5 fusion.85
  53.3 0.5 fusion.86
  53.8 0.5 fusion.87
  54.4 0.5 fusion.88
  54.9 0.5 fusion.89
  55.7 0.8 copy-done
  57.3 43.2 %all-reduce = (f32[16,16]{0,1:T(8,128)S(1)}, f32[16,16]{0,1:T(8,128)S(1)}, f32[16,16]{1,0:T(8,128)S(1)}, f32[16,16]{1,0:T(8,128)S(1)}) all-reduce(f32[16,16]{0,1:T(8,128)S(1)} %convolution_bitcast_fusion.4, f32[16,16]{0,1:T(8,128)S(1)} %bitcast.265, ...), channel_id=1, replica_groups=mesh['gx'=2,'gy'=4,'gz'=4] {'gx','gy','gz'}, use_global_device_ids=true, to_apply=%region_4.0 | all-reduce | flops 1024 | bytes 8192 | tf_op jit(solution)/shard_map/psum | solution.py:102
  100.6 1.5 cholesky.70
  102.1 0.6 compare_reduce_fusion.1
  102.8 0.6 fusion.56
  103.4 1.2 custom-call.10
  104.7 1.5 cholesky.59
  106.2 0.6 compare_reduce_fusion.2
  106.9 0.6 fusion.55
  107.5 1.2 custom-call.9
  110.8 4.2 %collective-permute-start.12 = (bf16[16,1,4,256]{3,0,2,1:T(8,128)(2,1)S(1)}, bf16[16,1,4,256]{3,0,2,1:T(8,128)(2,1)S(1)}, u32[]{:S(2)}, u32[]{:S(2)}) collective-permute-start(bf16[16,1,4,256]{3,0,2,1:T(8,128)(2,1)S(1)} %get-tuple-element.24), channel_id=1, source_target_pairs={{0,16},{1,17},{2,18},{3,19},{4,20},{5,21},{6,22},{7,23},{8,24},{9,... | collective-permute-start | bytes 98312 | tf_op jit(solution)/shard_map/ppermute | solution.py:19
  115.0 1.3 collective-permute-start.13
  116.6 4.2 %collective-permute-done.13 = bf16[16,1,4,256]{3,0,2,1:T(8,128)(2,1)S(1)} collective-permute-done((bf16[16,1,4,256]{3,0,2,1:T(8,128)(2,1)S(1)}, bf16[16,1,4,256]{3,0,2,1:T(8,128)(2,1)S(1)}, u32[]{:S(2)}, u32[]{:S(2)}) %collective-permute-start.13) | collective-permute-done | bytes 32800 | tf_op jit(solution)/shard_map/ppermute | solution.py:21
  120.8 1.3 collective-permute-start.14
  122.1 1.3 collective-permute-start.15
  123.5 2.1 %collective-permute-done.15 = bf16[16,4,1,256]{3,0,2,1:T(8,128)(2,1)S(1)} collective-permute-done((bf16[16,4,1,256]{3,0,2,1:T(8,128)(2,1)S(1)}, bf16[16,4,1,256]{3,0,2,1:T(8,128)(2,1)S(1)}, u32[]{:S(2)}, u32[]{:S(2)}) %collective-permute-start.15) | collective-permute-done | bytes 32800 | tf_op jit(solution)/shard_map/ppermute | solution.py:21
  125.7 2.3 %collective-permute-start.16 = (bf16[16,4,6,1]{3,0,2,1:T(8,128)(2,1)S(1)}, bf16[16,4,6,1]{3,0,2,1:T(8,128)(2,1)S(1)}, u32[]{:S(2)}, u32[]{:S(2)}) collective-permute-start(bf16[16,4,6,1]{3,0,2,1:T(8,128)(2,1)S(1)} %get-tuple-element.19), channel_id=1, source_target_pairs={{0,1},{1,2},{2,3},{4,5},{5,6},{6,7},{8,9},{9,10},{10,11},{12,13},{... | collective-permute-start | bytes 2312 | tf_op jit(solution)/shard_map/ppermute | solution.py:19
  128.1 1.3 collective-permute-start.17
  129.7 0.6 collective-permute-done.16
  130.3 4.3 %collective-permute-done.17 = bf16[16,4,6,1]{3,0,2,1:T(8,128)(2,1)S(1)} collective-permute-done((bf16[16,4,6,1]{3,0,2,1:T(8,128)(2,1)S(1)}, bf16[16,4,6,1]{3,0,2,1:T(8,128)(2,1)S(1)}, u32[]{:S(2)}, u32[]{:S(2)}) %collective-permute-start.17) | collective-permute-done | bytes 800 | tf_op jit(solution)/shard_map/ppermute | solution.py:21
  135.1 0.5 fusion.8
  135.6 0.5 fusion.10
  136.1 0.5 fusion.12
  137.2 0.5 fusion.16
  137.7 0.5 fusion.18
  138.2 0.5 fusion.20
  138.7 0.5 fusion.22
  140.0 39.1 %psum.39 = f32[16,16]{0,1:T(8,128)S(1)} all-reduce(f32[16,16]{0,1:T(8,128)S(1)} %convolution_bitcast_fusion.1), channel_id=1, replica_groups=mesh['gx'=2,'gy'=4,'gz'=4] {'gx','gy','gz'}, use_global_device_ids=true, to_apply=%region_7.10 | all-reduce | flops 256 | bytes 2048 | tf_op jit(solution)/shard_map/psum | solution.py:127
  179.3 1.5 cholesky.81
  180.7 0.6 compare_reduce_fusion
  181.4 0.6 fusion.57
  182.0 1.2 custom-call.11
  184.0 0.7 copy.45
  185.0 0.7 copy.44
  (101 shorter events, 8.5 us)
Async XLA Ops:
  1.4 13.0 %collective-permute-start.6 = (f32[1,4,256]{2,1,0:T(4,128)S(1)}, f32[1,4,256]{2,1,0:T(4,128)S(1)}, u32[]{:S(2)}, u32[]{:S(2)}) collective-permute-start(f32[1,4,256]{2,1,0:T(4,128)S(1)} %get-tuple-element.42), channel_id=1, source_target_pairs={{0,16},{1,17},{2,18},{3,19},{4,20},{5,21},{6,22},{7,23},{8,24},{9,... | collective-permute-start | bytes 12296 | tf_op jit(solution)/shard_map/ppermute | solution.py:19
  6.4 8.1 %collective-permute-start.7 = (f32[1,4,256]{2,1,0:T(4,128)S(1)}, f32[1,4,256]{2,1,0:T(4,128)S(1)}, u32[]{:S(2)}, u32[]{:S(2)}) collective-permute-start(f32[1,4,256]{2,1,0:T(4,128)S(1)} %get-tuple-element.43), channel_id=1, source_target_pairs={{16,0},{17,1},{18,2},{19,3},{20,4},{21,5},{22,6},{23,7},{24,8},{25... | collective-permute-start | bytes 12296 | tf_op jit(solution)/shard_map/ppermute | solution.py:21
  8.6 21.3 %collective-permute-start = (bf16[16,1,4,256]{3,2,1,0:T(4,128)(2,1)S(1)}, bf16[16,1,4,256]{3,2,1,0:T(4,128)(2,1)S(1)}, u32[]{:S(2)}, u32[]{:S(2)}) collective-permute-start(bf16[16,1,4,256]{3,2,1,0:T(4,128)(2,1)S(1)} %get-tuple-element.26), channel_id=1, source_target_pairs={{0,16},{1,17},{2,18},{3,19},{4,20},{5,21},{6,22},{7,23},{8,24},{9,... | collective-permute-start | bytes 98312 | tf_op jit(solution)/shard_map/ppermute | solution.py:19
  13.2 16.8 %collective-permute-start.1 = (bf16[16,1,4,256]{3,2,1,0:T(4,128)(2,1)S(1)}, bf16[16,1,4,256]{3,2,1,0:T(4,128)(2,1)S(1)}, u32[]{:S(2)}, u32[]{:S(2)}) collective-permute-start(bf16[16,1,4,256]{3,2,1,0:T(4,128)(2,1)S(1)} %get-tuple-element.27), channel_id=1, source_target_pairs={{16,0},{17,1},{18,2},{19,3},{20,4},{21,5},{22,6},{23,7},{24,8},{25... | collective-permute-start | bytes 98312 | tf_op jit(solution)/shard_map/ppermute | solution.py:21
  14.5 3.9 %collective-permute-start.8 = (f32[4,1,256]{2,1,0:T(1,128)S(1)}, f32[4,1,256]{2,1,0:T(1,128)S(1)}, u32[]{:S(2)}, u32[]{:S(2)}) collective-permute-start(f32[4,1,256]{2,1,0:T(1,128)S(1)} %get-tuple-element.40), channel_id=1, source_target_pairs={{0,4},{4,8},{8,12},{1,5},{5,9},{9,13},{2,6},{6,10},{10,14},{3,7},{... | collective-permute-start | bytes 12296 | tf_op jit(solution)/shard_map/ppermute | solution.py:19
  15.8 4.8 %collective-permute-start.9 = (f32[4,1,256]{2,1,0:T(1,128)S(1)}, f32[4,1,256]{2,1,0:T(1,128)S(1)}, u32[]{:S(2)}, u32[]{:S(2)}) collective-permute-start(f32[4,1,256]{2,1,0:T(1,128)S(1)} %get-tuple-element.41), channel_id=1, source_target_pairs={{4,0},{8,4},{12,8},{5,1},{9,5},{13,9},{6,2},{10,6},{14,10},{7,3},{... | collective-permute-start | bytes 12296 | tf_op jit(solution)/shard_map/ppermute | solution.py:21
  20.7 4.9 %collective-permute-start.10 = (f32[4,6,1]{2,1,0:T(8,128)S(1)}, f32[4,6,1]{2,1,0:T(8,128)S(1)}, u32[]{:S(2)}, u32[]{:S(2)}) collective-permute-start(f32[4,6,1]{2,1,0:T(8,128)S(1)} %get-tuple-element.36), channel_id=1, source_target_pairs={{0,1},{1,2},{2,3},{4,5},{5,6},{6,7},{8,9},{9,10},{10,11},{12,13},{... | collective-permute-start | bytes 296 | tf_op jit(solution)/shard_map/ppermute | solution.py:19
  24.2 5.6 %collective-permute-start.11 = (f32[4,6,1]{2,1,0:T(8,128)S(1)}, f32[4,6,1]{2,1,0:T(8,128)S(1)}, u32[]{:S(2)}, u32[]{:S(2)}) collective-permute-start(f32[4,6,1]{2,1,0:T(8,128)S(1)} %get-tuple-element.37), channel_id=1, source_target_pairs={{1,0},{2,1},{3,2},{5,4},{6,5},{7,6},{9,8},{10,9},{11,10},{13,12},{... | collective-permute-start | bytes 296 | tf_op jit(solution)/shard_map/ppermute | solution.py:21
  30.1 4.2 %collective-permute-start.2 = (bf16[16,4,1,256]{3,2,1,0:T(2,128)(2,1)S(1)}, bf16[16,4,1,256]{3,2,1,0:T(2,128)(2,1)S(1)}, u32[]{:S(2)}, u32[]{:S(2)}) collective-permute-start(bf16[16,4,1,256]{3,2,1,0:T(2,128)(2,1)S(1)} %get-tuple-element.22), channel_id=1, source_target_pairs={{0,4},{4,8},{8,12},{1,5},{5,9},{9,13},{2,6},{6,10},{10,14},{3,7},{... | collective-permute-start | bytes 98312 | tf_op jit(solution)/shard_map/ppermute | solution.py:19
  33.0 4.2 %collective-permute-start.3 = (bf16[16,4,1,256]{3,2,1,0:T(2,128)(2,1)S(1)}, bf16[16,4,1,256]{3,2,1,0:T(2,128)(2,1)S(1)}, u32[]{:S(2)}, u32[]{:S(2)}) collective-permute-start(bf16[16,4,1,256]{3,2,1,0:T(2,128)(2,1)S(1)} %get-tuple-element.23), channel_id=1, source_target_pairs={{4,0},{8,4},{12,8},{5,1},{9,5},{13,9},{6,2},{10,6},{14,10},{7,3},{... | collective-permute-start | bytes 98312 | tf_op jit(solution)/shard_map/ppermute | solution.py:21
  37.5 6.0 %collective-permute-start.4 = (bf16[16,4,6,1]{3,2,1,0:T(8,128)(2,1)S(1)}, bf16[16,4,6,1]{3,2,1,0:T(8,128)(2,1)S(1)}, u32[]{:S(2)}, u32[]{:S(2)}) collective-permute-start(bf16[16,4,6,1]{3,2,1,0:T(8,128)(2,1)S(1)} %get-tuple-element.15), channel_id=1, source_target_pairs={{0,1},{1,2},{2,3},{4,5},{5,6},{6,7},{8,9},{9,10},{10,11},{12,13},{... | collective-permute-start | bytes 2312 | tf_op jit(solution)/shard_map/ppermute | solution.py:19
  41.0 6.9 %collective-permute-start.5 = (bf16[16,4,6,1]{3,2,1,0:T(8,128)(2,1)S(1)}, bf16[16,4,6,1]{3,2,1,0:T(8,128)(2,1)S(1)}, u32[]{:S(2)}, u32[]{:S(2)}) collective-permute-start(bf16[16,4,6,1]{3,2,1,0:T(8,128)(2,1)S(1)} %get-tuple-element.14), channel_id=1, source_target_pairs={{1,0},{2,1},{3,2},{5,4},{6,5},{7,6},{9,8},{10,9},{11,10},{13,12},{... | collective-permute-start | bytes 2312 | tf_op jit(solution)/shard_map/ppermute | solution.py:21
  49.3 1.6 copy-start.1
  51.0 0.7 copy-start.2
  51.0 1.2 copy-start.3
  51.6 1.1 copy-start.4
  52.2 1.1 copy-start.5
  52.7 1.1 copy-start.6
  53.3 1.1 copy-start.7
  53.8 1.1 copy-start.8
  55.6 0.9 copy-start
  110.8 5.8 %collective-permute-start.12 = (bf16[16,1,4,256]{3,0,2,1:T(8,128)(2,1)S(1)}, bf16[16,1,4,256]{3,0,2,1:T(8,128)(2,1)S(1)}, u32[]{:S(2)}, u32[]{:S(2)}) collective-permute-start(bf16[16,1,4,256]{3,0,2,1:T(8,128)(2,1)S(1)} %get-tuple-element.24), channel_id=1, source_target_pairs={{0,16},{1,17},{2,18},{3,19},{4,20},{5,21},{6,22},{7,23},{8,24},{9,... | collective-permute-start | bytes 98312 | tf_op jit(solution)/shard_map/ppermute | solution.py:19
  115.0 5.8 %collective-permute-start.13 = (bf16[16,1,4,256]{3,0,2,1:T(8,128)(2,1)S(1)}, bf16[16,1,4,256]{3,0,2,1:T(8,128)(2,1)S(1)}, u32[]{:S(2)}, u32[]{:S(2)}) collective-permute-start(bf16[16,1,4,256]{3,0,2,1:T(8,128)(2,1)S(1)} %get-tuple-element.25), channel_id=1, source_target_pairs={{16,0},{17,1},{18,2},{19,3},{20,4},{21,5},{22,6},{23,7},{24,8},{25... | collective-permute-start | bytes 98312 | tf_op jit(solution)/shard_map/ppermute | solution.py:21
  120.8 2.6 %collective-permute-start.14 = (bf16[16,4,1,256]{3,0,2,1:T(8,128)(2,1)S(1)}, bf16[16,4,1,256]{3,0,2,1:T(8,128)(2,1)S(1)}, u32[]{:S(2)}, u32[]{:S(2)}) collective-permute-start(bf16[16,4,1,256]{3,0,2,1:T(8,128)(2,1)S(1)} %get-tuple-element.20), channel_id=1, source_target_pairs={{0,4},{4,8},{8,12},{1,5},{5,9},{9,13},{2,6},{6,10},{10,14},{3,7},{... | collective-permute-start | bytes 98312 | tf_op jit(solution)/shard_map/ppermute | solution.py:19
  122.1 3.5 %collective-permute-start.15 = (bf16[16,4,1,256]{3,0,2,1:T(8,128)(2,1)S(1)}, bf16[16,4,1,256]{3,0,2,1:T(8,128)(2,1)S(1)}, u32[]{:S(2)}, u32[]{:S(2)}) collective-permute-start(bf16[16,4,1,256]{3,0,2,1:T(8,128)(2,1)S(1)} %get-tuple-element.21), channel_id=1, source_target_pairs={{4,0},{8,4},{12,8},{5,1},{9,5},{13,9},{6,2},{10,6},{14,10},{7,3},{... | collective-permute-start | bytes 98312 | tf_op jit(solution)/shard_map/ppermute | solution.py:21
  125.7 4.5 %collective-permute-start.16 = (bf16[16,4,6,1]{3,0,2,1:T(8,128)(2,1)S(1)}, bf16[16,4,6,1]{3,0,2,1:T(8,128)(2,1)S(1)}, u32[]{:S(2)}, u32[]{:S(2)}) collective-permute-start(bf16[16,4,6,1]{3,0,2,1:T(8,128)(2,1)S(1)} %get-tuple-element.19), channel_id=1, source_target_pairs={{0,1},{1,2},{2,3},{4,5},{5,6},{6,7},{8,9},{9,10},{10,11},{12,13},{... | collective-permute-start | bytes 2312 | tf_op jit(solution)/shard_map/ppermute | solution.py:19
  128.1 6.5 %collective-permute-start.17 = (bf16[16,4,6,1]{3,0,2,1:T(8,128)(2,1)S(1)}, bf16[16,4,6,1]{3,0,2,1:T(8,128)(2,1)S(1)}, u32[]{:S(2)}, u32[]{:S(2)}) collective-permute-start(bf16[16,4,6,1]{3,0,2,1:T(8,128)(2,1)S(1)} %get-tuple-element.18), channel_id=1, source_target_pairs={{1,0},{2,1},{3,2},{5,4},{6,5},{7,6},{9,8},{10,9},{11,10},{13,12},{... | collective-permute-start | bytes 2312 | tf_op jit(solution)/shard_map/ppermute | solution.py:21
where the time goes:
time: 187 us; the launch traced here: 186 us
  blocking collectives  82.4 us (44%)
  starting transfers between devices  40 us (21%)
  waiting for transfers between devices  26.4 us (14%)
  other arithmetic  15.8 us (8%)
  matrix products  13.6 us (7%)
  local copies, waits for them, and re-layouts  6.08 us (3%)
    psum x1, blocking collectives, residual_gram(): return lax.psum(local_gram(residual, residual), ('gx', 'gy', 'gz'))  43.2 us
    psum x1, blocking collectives, on_device(): lax.psum((local_gram(direction, image), local_gram(image, residual), loca...  39.1 us
    ppermute x9, starting transfers between devices, padded_2(): lax.ppermute(tail, axis, [(i, (i + 1) % count) for i in range(ends)])  28.4 us
    ppermute x9, waiting for transfers between devices, padded_2(): lax.ppermute(head, axis, [((i + 1) % count, i) for i in range(ends)])  24.2 us
    ppermute x9, starting transfers between devices, padded_2(): lax.ppermute(head, axis, [((i + 1) % count, i) for i in range(ends)])  11.6 us
    dot_general x16, matrix products, apply_operator(): jnp.einsum('b,bcxyz->cxyz', kernel[corner], stacked, preferred_element_ty...  8.36 us
    another operation x9, other arithmetic, solve_small(): factor = jnp.linalg.cholesky(matrix)  6.4 us
    another operation x6, other arithmetic, solve_small(): return jax.scipy.linalg.cho_solve((factor, True), rhs_small)  5.63 us
  transfers between devices with their start and end apart: 18, of which 12 were waited for; matrix products, arithmetic and copies ran while one was open for 2% of the time, Pallas kernels for 0%

commit v1 on v0

--- a/solution.py
+++ b/solution.py
@@ -99,7 +99,7 @@
 
 
 def residual_gram(residual):
-    return lax.psum(local_gram(residual, residual), ("gx", "gy", "gz"))
+    return jnp.sum(lax.all_gather(local_gram(residual, residual), ("gx", "gy", "gz")), axis=0)
 
 
 def on_device(loads, moduli, material):

time: 187 us -> 248 us (1.33)
  blocking collectives: 82.4 us -> 152 us
  starting transfers between devices: 40 us -> 34.8 us
  waiting for transfers between devices: 26.4 us -> 23.4 us
    all_gather x0 -> x1, blocking collectives: none -> 70.4 us  [residual_gram(): lax.all_gather(local_gram(residual, residual), ('gx', 'gy', 'gz'))]
    psum x1 -> x0, blocking collectives: 43.2 us -> none  [residual_gram(): return lax.psum(local_gram(residual, residual), ('gx', 'gy', 'gz'))]
    psum x1 -> x2, blocking collectives: 39.1 us -> 82 us  [on_device(): lax.psum((local_gram(direction, image), local_gram(image, residual), loca...]
    ppermute x9, starting transfers between devices: 28.4 us -> 23.2 us  [padded_2(): lax.ppermute(tail, axis, [(i, (i + 1) % count) for i in range(ends)])]
    ppermute x9, waiting for transfers between devices: 24.2 us -> 21.3 us  [padded_2(): lax.ppermute(head, axis, [((i + 1) % count, i) for i in range(ends)])]
  transfers between devices with their start and end apart: 18 -> 18, of which waited for: 12 -> 10; matrix products, arithmetic and copies ran while one was open for 2% -> 3% of each run, Pallas kernels for 0% -> 0%
where the time goes in v1:
time: 248 us; the launch traced here: 247 us
  blocking collectives  152 us (61%)
  starting transfers between devices  34.8 us (14%)
  waiting for transfers between devices  23.4 us (9%)
  other arithmetic  15.9 us (6%)
  matrix products  13.6 us (5%)
  local copies, waits for them, and re-layouts  6.08 us (2%)
    psum x2, blocking collectives, on_device(): lax.psum((local_gram(direction, image), local_gram(image, residual), loca...  82 us
    all_gather x1, blocking collectives, residual_gram(): lax.all_gather(local_gram(residual, residual), ('gx', 'gy', 'gz'))  70.4 us
    ppermute x9, starting transfers between devices, padded_2(): lax.ppermute(tail, axis, [(i, (i + 1) % count) for i in range(ends)])  23.2 us
    ppermute x9, waiting for transfers between devices, padded_2(): lax.ppermute(head, axis, [((i + 1) % count, i) for i in range(ends)])  21.3 us
    ppermute x9, starting transfers between devices, padded_2(): lax.ppermute(head, axis, [((i + 1) % count, i) for i in range(ends)])  11.6 us
    dot_general x16, matrix products, apply_operator(): jnp.einsum('b,bcxyz->cxyz', kernel[corner], stacked, preferred_element_ty...  8.36 us
    another operation x9, other arithmetic, solve_small(): factor = jnp.linalg.cholesky(matrix)  6.39 us
    another operation x6, other arithmetic, solve_small(): return jax.scipy.linalg.cho_solve((factor, True), rhs_small)  5.63 us
  transfers between devices with their start and end apart: 18, of which 10 were waited for; matrix products, arithmetic and copies ran while one was open for 3% of the time, Pallas kernels for 0%

profile of v1, /device:TPU:0, one launch (start us, length us, event | category | flops | bytes accessed | tf_op | source)
XLA Modules:
  0.0 247.5 jit_solution(8738203187544206116)
XLA Ops:
  0.6 0.9 convert_element_type.9
  1.6 4.9 %collective-permute-start = (bf16[16,1,4,256]{3,2,1,0:T(4,128)(2,1)S(1)}, bf16[16,1,4,256]{3,2,1,0:T(4,128)(2,1)S(1)}, u32[]{:S(2)}, u32[]{:S(2)}) collective-permute-start(bf16[16,1,4,256]{3,2,1,0:T(4,128)(2,1)S(1)} %get-tuple-element.27), channel_id=1, source_target_pairs={{0,16},{1,17},{2,18},{3,19},{4,20},{5,21},{6,22},{7,23},{8,24},{9,... | collective-permute-start | bytes 98312 | tf_op jit(solution)/shard_map/ppermute | solution.py:19
  6.5 1.3 collective-permute-start.1
  7.8 0.8 select_reduce_fusion
  8.6 4.5 %collective-permute-start.6 = (f32[1,4,256]{2,1,0:T(4,128)S(1)}, f32[1,4,256]{2,1,0:T(4,128)S(1)}, u32[]{:S(2)}, u32[]{:S(2)}) collective-permute-start(f32[1,4,256]{2,1,0:T(4,128)S(1)} %get-tuple-element.43), channel_id=1, source_target_pairs={{0,16},{1,17},{2,18},{3,19},{4,20},{5,21},{6,22},{7,23},{8,24},{9,... | collective-permute-start | bytes 12296 | tf_op jit(solution)/shard_map/ppermute | solution.py:19
  13.2 1.3 collective-permute-start.7
  14.5 1.3 convolution_bitcast_fusion.4
  15.7 70.4 %all-gather = f32[512,16]{1,0:T(8,128)S(1)} all-gather(f32[16,16]{1,0:T(8,128)S(1)} %convolution_bitcast_fusion.4), channel_id=2, replica_groups=mesh['gx'=2,'gy'=4,'gz'=4] {'gx','gy','gz'}, dimensions={0}, use_global_device_ids=true | all-gather | bytes 33792 | tf_op jit(solution)/shard_map/all_gather | solution.py:102
  86.3 1.5 cholesky.70
  87.7 0.6 compare_reduce_fusion.1
  88.4 1.3 collective-permute-start.8
  89.7 1.3 collective-permute-start.9
  91.0 0.7 fusion.56
  91.7 1.2 custom-call.10
  93.0 1.3 collective-permute-start.10
  94.3 1.3 collective-permute-start.11
  95.7 4.2 %collective-permute-done.11 = f32[4,6,1]{2,1,0:T(8,128)S(1)} collective-permute-done((f32[4,6,1]{2,1,0:T(8,128)S(1)}, f32[4,6,1]{2,1,0:T(8,128)S(1)}, u32[]{:S(2)}, u32[]{:S(2)}) %collective-permute-start.11) | collective-permute-done | bytes 128 | tf_op jit(solution)/shard_map/ppermute | solution.py:21
  100.3 2.0 collective-permute-start.2
  102.3 1.3 collective-permute-start.3
  103.7 1.8 collective-permute-done.3
  105.8 1.8 collective-permute-start.4
  107.6 1.3 collective-permute-start.5
  109.0 1.1 collective-permute-done.4
  110.1 4.6 %collective-permute-done.5 = bf16[16,4,6,1]{3,2,1,0:T(8,128)(2,1)S(1)} collective-permute-done((bf16[16,4,6,1]{3,2,1,0:T(8,128)(2,1)S(1)}, bf16[16,4,6,1]{3,2,1,0:T(8,128)(2,1)S(1)}, u32[]{:S(2)}, u32[]{:S(2)}) %collective-permute-start.5) | collective-permute-done | bytes 800 | tf_op jit(solution)/shard_map/ppermute | solution.py:21
  114.7 0.9 pad_maximum_fusion
  116.1 1.6 copy.66
  117.8 0.5 fusion.82
  118.4 0.5 fusion.83
  119.0 0.5 fusion.84
  119.5 0.5 fusion.85
  120.1 0.5 fusion.86
  120.7 0.5 fusion.87
  121.2 0.5 fusion.88
  121.7 0.5 fusion.89
  122.6 0.8 copy-done
  124.1 42.3 %all-reduce = (f32[16,16]{0,1:T(8,128)S(1)}, f32[16,16]{1,0:T(8,128)S(1)}, f32[16,16]{1,0:T(8,128)S(1)}) all-reduce(f32[16,16]{0,1:T(8,128)S(1)} %bitcast.269, f32[16,16]{1,0:T(8,128)S(1)} %convolution_bitcast_fusion.3, f32[16,16]{1,0:T(8,128)S(1)} %bitcast.270), channel_id=1, replica_groups=mesh['gx'=2,'gy'=4,'gz'=4] {'gx','gy','gz'}, use_global_device_ids=true, to_apply=%region_1.2 | all-reduce | flops 768 | bytes 6144 | tf_op jit(solution)/shard_map/psum | solution.py:127
  166.5 1.5 cholesky.59
  168.0 0.6 compare_reduce_fusion.2
  168.6 0.6 fusion.55
  169.3 1.2 custom-call.9
  172.6 4.2 %collective-permute-start.12 = (bf16[16,1,4,256]{3,0,2,1:T(8,128)(2,1)S(1)}, bf16[16,1,4,256]{3,0,2,1:T(8,128)(2,1)S(1)}, u32[]{:S(2)}, u32[]{:S(2)}) collective-permute-start(bf16[16,1,4,256]{3,0,2,1:T(8,128)(2,1)S(1)} %get-tuple-element.25), channel_id=1, source_target_pairs={{0,16},{1,17},{2,18},{3,19},{4,20},{5,21},{6,22},{7,23},{8,24},{9,... | collective-permute-start | bytes 98312 | tf_op jit(solution)/shard_map/ppermute | solution.py:19
  176.8 1.3 collective-permute-start.13
  178.4 4.2 %collective-permute-done.13 = bf16[16,1,4,256]{3,0,2,1:T(8,128)(2,1)S(1)} collective-permute-done((bf16[16,1,4,256]{3,0,2,1:T(8,128)(2,1)S(1)}, bf16[16,1,4,256]{3,0,2,1:T(8,128)(2,1)S(1)}, u32[]{:S(2)}, u32[]{:S(2)}) %collective-permute-start.13) | collective-permute-done | bytes 32800 | tf_op jit(solution)/shard_map/ppermute | solution.py:21
  182.6 1.3 collective-permute-start.14
  183.9 1.3 collective-permute-start.15
  185.2 2.1 collective-permute-done.15
  187.5 1.8 collective-permute-start.16
  189.4 1.3 collective-permute-start.17
  191.0 0.6 collective-permute-done.16
  191.6 4.3 %collective-permute-done.17 = bf16[16,4,6,1]{3,0,2,1:T(8,128)(2,1)S(1)} collective-permute-done((bf16[16,4,6,1]{3,0,2,1:T(8,128)(2,1)S(1)}, bf16[16,4,6,1]{3,0,2,1:T(8,128)(2,1)S(1)}, u32[]{:S(2)}, u32[]{:S(2)}) %collective-permute-start.17) | collective-permute-done | bytes 800 | tf_op jit(solution)/shard_map/ppermute | solution.py:21
  196.3 0.5 fusion.8
  196.9 0.5 fusion.10
  197.4 0.5 fusion.12
  198.4 0.5 fusion.16
  199.0 0.5 fusion.18
  199.5 0.5 fusion.20
  200.0 0.5 fusion.22
  201.3 39.7 %psum.31 = f32[16,16]{0,1:T(8,128)S(1)} all-reduce(f32[16,16]{0,1:T(8,128)S(1)} %convolution_bitcast_fusion.1), channel_id=1, replica_groups=mesh['gx'=2,'gy'=4,'gz'=4] {'gx','gy','gz'}, use_global_device_ids=true, to_apply=%region_7.10 | all-reduce | flops 256 | bytes 2048 | tf_op jit(solution)/shard_map/psum | solution.py:127
  241.1 1.5 cholesky.81
  242.5 0.6 compare_reduce_fusion
  243.2 0.6 fusion.57
  243.8 1.2 custom-call.11
  245.8 0.7 copy.65
  246.8 0.7 copy.64
  (103 shorter events, 8.5 us)
Async XLA Ops:
  1.6 98.5 %collective-permute-start = (bf16[16,1,4,256]{3,2,1,0:T(4,128)(2,1)S(1)}, bf16[16,1,4,256]{3,2,1,0:T(4,128)(2,1)S(1)}, u32[]{:S(2)}, u32[]{:S(2)}) collective-permute-start(bf16[16,1,4,256]{3,2,1,0:T(4,128)(2,1)S(1)} %get-tuple-element.27), channel_id=1, source_target_pairs={{0,16},{1,17},{2,18},{3,19},{4,20},{5,21},{6,22},{7,23},{8,24},{9,... | collective-permute-start | bytes 98312 | tf_op jit(solution)/shard_map/ppermute | solution.py:19
  6.5 93.6 %collective-permute-start.1 = (bf16[16,1,4,256]{3,2,1,0:T(4,128)(2,1)S(1)}, bf16[16,1,4,256]{3,2,1,0:T(4,128)(2,1)S(1)}, u32[]{:S(2)}, u32[]{:S(2)}) collective-permute-start(bf16[16,1,4,256]{3,2,1,0:T(4,128)(2,1)S(1)} %get-tuple-element.28), channel_id=1, source_target_pairs={{16,0},{17,1},{18,2},{19,3},{20,4},{21,5},{22,6},{23,7},{24,8},{25... | collective-permute-start | bytes 98312 | tf_op jit(solution)/shard_map/ppermute | solution.py:21
  8.6 79.8 %collective-permute-start.6 = (f32[1,4,256]{2,1,0:T(4,128)S(1)}, f32[1,4,256]{2,1,0:T(4,128)S(1)}, u32[]{:S(2)}, u32[]{:S(2)}) collective-permute-start(f32[1,4,256]{2,1,0:T(4,128)S(1)} %get-tuple-element.43), channel_id=1, source_target_pairs={{0,16},{1,17},{2,18},{3,19},{4,20},{5,21},{6,22},{7,23},{8,24},{9,... | collective-permute-start | bytes 12296 | tf_op jit(solution)/shard_map/ppermute | solution.py:19
  13.2 75.2 %collective-permute-start.7 = (f32[1,4,256]{2,1,0:T(4,128)S(1)}, f32[1,4,256]{2,1,0:T(4,128)S(1)}, u32[]{:S(2)}, u32[]{:S(2)}) collective-permute-start(f32[1,4,256]{2,1,0:T(4,128)S(1)} %get-tuple-element.44), channel_id=1, source_target_pairs={{16,0},{17,1},{18,2},{19,3},{20,4},{21,5},{22,6},{23,7},{24,8},{25... | collective-permute-start | bytes 12296 | tf_op jit(solution)/shard_map/ppermute | solution.py:21
  88.4 4.5 %collective-permute-start.8 = (f32[4,1,256]{2,1,0:T(1,128)S(1)}, f32[4,1,256]{2,1,0:T(1,128)S(1)}, u32[]{:S(2)}, u32[]{:S(2)}) collective-permute-start(f32[4,1,256]{2,1,0:T(1,128)S(1)} %get-tuple-element.41), channel_id=1, source_target_pairs={{0,4},{4,8},{8,12},{1,5},{5,9},{9,13},{2,6},{6,10},{10,14},{3,7},{... | collective-permute-start | bytes 12296 | tf_op jit(solution)/shard_map/ppermute | solution.py:19
  89.7 3.2 %collective-permute-start.9 = (f32[4,1,256]{2,1,0:T(1,128)S(1)}, f32[4,1,256]{2,1,0:T(1,128)S(1)}, u32[]{:S(2)}, u32[]{:S(2)}) collective-permute-start(f32[4,1,256]{2,1,0:T(1,128)S(1)} %get-tuple-element.42), channel_id=1, source_target_pairs={{4,0},{8,4},{12,8},{5,1},{9,5},{13,9},{6,2},{10,6},{14,10},{7,3},{... | collective-permute-start | bytes 12296 | tf_op jit(solution)/shard_map/ppermute | solution.py:21
  93.0 2.7 %collective-permute-start.10 = (f32[4,6,1]{2,1,0:T(8,128)S(1)}, f32[4,6,1]{2,1,0:T(8,128)S(1)}, u32[]{:S(2)}, u32[]{:S(2)}) collective-permute-start(f32[4,6,1]{2,1,0:T(8,128)S(1)} %get-tuple-element.37), channel_id=1, source_target_pairs={{0,1},{1,2},{2,3},{4,5},{5,6},{6,7},{8,9},{9,10},{10,11},{12,13},{... | collective-permute-start | bytes 296 | tf_op jit(solution)/shard_map/ppermute | solution.py:19
  94.3 5.6 %collective-permute-start.11 = (f32[4,6,1]{2,1,0:T(8,128)S(1)}, f32[4,6,1]{2,1,0:T(8,128)S(1)}, u32[]{:S(2)}, u32[]{:S(2)}) collective-permute-start(f32[4,6,1]{2,1,0:T(8,128)S(1)} %get-tuple-element.38), channel_id=1, source_target_pairs={{1,0},{2,1},{3,2},{5,4},{6,5},{7,6},{9,8},{10,9},{11,10},{13,12},{... | collective-permute-start | bytes 296 | tf_op jit(solution)/shard_map/ppermute | solution.py:21
  100.3 3.4 %collective-permute-start.2 = (bf16[16,4,1,256]{3,2,1,0:T(2,128)(2,1)S(1)}, bf16[16,4,1,256]{3,2,1,0:T(2,128)(2,1)S(1)}, u32[]{:S(2)}, u32[]{:S(2)}) collective-permute-start(bf16[16,4,1,256]{3,2,1,0:T(2,128)(2,1)S(1)} %get-tuple-element.23), channel_id=1, source_target_pairs={{0,4},{4,8},{8,12},{1,5},{5,9},{9,13},{2,6},{6,10},{10,14},{3,7},{... | collective-permute-start | bytes 98312 | tf_op jit(solution)/shard_map/ppermute | solution.py:19
  102.3 3.1 %collective-permute-start.3 = (bf16[16,4,1,256]{3,2,1,0:T(2,128)(2,1)S(1)}, bf16[16,4,1,256]{3,2,1,0:T(2,128)(2,1)S(1)}, u32[]{:S(2)}, u32[]{:S(2)}) collective-permute-start(bf16[16,4,1,256]{3,2,1,0:T(2,128)(2,1)S(1)} %get-tuple-element.24), channel_id=1, source_target_pairs={{4,0},{8,4},{12,8},{5,1},{9,5},{13,9},{6,2},{10,6},{14,10},{7,3},{... | collective-permute-start | bytes 98312 | tf_op jit(solution)/shard_map/ppermute | solution.py:21
  105.8 4.3 %collective-permute-start.4 = (bf16[16,4,6,1]{3,2,1,0:T(8,128)(2,1)S(1)}, bf16[16,4,6,1]{3,2,1,0:T(8,128)(2,1)S(1)}, u32[]{:S(2)}, u32[]{:S(2)}) collective-permute-start(bf16[16,4,6,1]{3,2,1,0:T(8,128)(2,1)S(1)} %get-tuple-element.16), channel_id=1, source_target_pairs={{0,1},{1,2},{2,3},{4,5},{5,6},{6,7},{8,9},{9,10},{10,11},{12,13},{... | collective-permute-start | bytes 2312 | tf_op jit(solution)/shard_map/ppermute | solution.py:19
  107.6 7.1 %collective-permute-start.5 = (bf16[16,4,6,1]{3,2,1,0:T(8,128)(2,1)S(1)}, bf16[16,4,6,1]{3,2,1,0:T(8,128)(2,1)S(1)}, u32[]{:S(2)}, u32[]{:S(2)}) collective-permute-start(bf16[16,4,6,1]{3,2,1,0:T(8,128)(2,1)S(1)} %get-tuple-element.15), channel_id=1, source_target_pairs={{1,0},{2,1},{3,2},{5,4},{6,5},{7,6},{9,8},{10,9},{11,10},{13,12},{... | collective-permute-start | bytes 2312 | tf_op jit(solution)/shard_map/ppermute | solution.py:21
  116.1 1.6 copy-start.1
  117.8 0.7 copy-start.2
  117.8 1.2 copy-start.3
  118.4 1.1 copy-start.4
  119.0 1.1 copy-start.5
  119.5 1.1 copy-start.6
  120.1 1.1 copy-start.7
  120.6 1.1 copy-start.8
  122.4 0.9 copy-start
  172.6 5.8 %collective-permute-start.12 = (bf16[16,1,4,256]{3,0,2,1:T(8,128)(2,1)S(1)}, bf16[16,1,4,256]{3,0,2,1:T(8,128)(2,1)S(1)}, u32[]{:S(2)}, u32[]{:S(2)}) collective-permute-start(bf16[16,1,4,256]{3,0,2,1:T(8,128)(2,1)S(1)} %get-tuple-element.25), channel_id=1, source_target_pairs={{0,16},{1,17},{2,18},{3,19},{4,20},{5,21},{6,22},{7,23},{8,24},{9,... | collective-permute-start | bytes 98312 | tf_op jit(solution)/shard_map/ppermute | solution.py:19
  176.8 5.8 %collective-permute-start.13 = (bf16[16,1,4,256]{3,0,2,1:T(8,128)(2,1)S(1)}, bf16[16,1,4,256]{3,0,2,1:T(8,128)(2,1)S(1)}, u32[]{:S(2)}, u32[]{:S(2)}) collective-permute-start(bf16[16,1,4,256]{3,0,2,1:T(8,128)(2,1)S(1)} %get-tuple-element.26), channel_id=1, source_target_pairs={{16,0},{17,1},{18,2},{19,3},{20,4},{21,5},{22,6},{23,7},{24,8},{25... | collective-permute-start | bytes 98312 | tf_op jit(solution)/shard_map/ppermute | solution.py:21
  182.6 2.6 %collective-permute-start.14 = (bf16[16,4,1,256]{3,0,2,1:T(8,128)(2,1)S(1)}, bf16[16,4,1,256]{3,0,2,1:T(8,128)(2,1)S(1)}, u32[]{:S(2)}, u32[]{:S(2)}) collective-permute-start(bf16[16,4,1,256]{3,0,2,1:T(8,128)(2,1)S(1)} %get-tuple-element.21), channel_id=1, source_target_pairs={{0,4},{4,8},{8,12},{1,5},{5,9},{9,13},{2,6},{6,10},{10,14},{3,7},{... | collective-permute-start | bytes 98312 | tf_op jit(solution)/shard_map/ppermute | solution.py:19
  183.9 3.4 %collective-permute-start.15 = (bf16[16,4,1,256]{3,0,2,1:T(8,128)(2,1)S(1)}, bf16[16,4,1,256]{3,0,2,1:T(8,128)(2,1)S(1)}, u32[]{:S(2)}, u32[]{:S(2)}) collective-permute-start(bf16[16,4,1,256]{3,0,2,1:T(8,128)(2,1)S(1)} %get-tuple-element.22), channel_id=1, source_target_pairs={{4,0},{8,4},{12,8},{5,1},{9,5},{13,9},{6,2},{10,6},{14,10},{7,3},{... | collective-permute-start | bytes 98312 | tf_op jit(solution)/shard_map/ppermute | solution.py:21
  187.5 4.0 %collective-permute-start.16 = (bf16[16,4,6,1]{3,0,2,1:T(8,128)(2,1)S(1)}, bf16[16,4,6,1]{3,0,2,1:T(8,128)(2,1)S(1)}, u32[]{:S(2)}, u32[]{:S(2)}) collective-permute-start(bf16[16,4,6,1]{3,0,2,1:T(8,128)(2,1)S(1)} %get-tuple-element.20), channel_id=1, source_target_pairs={{0,1},{1,2},{2,3},{4,5},{5,6},{6,7},{8,9},{9,10},{10,11},{12,13},{... | collective-permute-start | bytes 2312 | tf_op jit(solution)/shard_map/ppermute | solution.py:19
  189.4 6.5 %collective-permute-start.17 = (bf16[16,4,6,1]{3,0,2,1:T(8,128)(2,1)S(1)}, bf16[16,4,6,1]{3,0,2,1:T(8,128)(2,1)S(1)}, u32[]{:S(2)}, u32[]{:S(2)}) collective-permute-start(bf16[16,4,6,1]{3,0,2,1:T(8,128)(2,1)S(1)} %get-tuple-element.19), channel_id=1, source_target_pairs={{1,0},{2,1},{3,2},{5,4},{6,5},{7,6},{9,8},{10,9},{11,10},{13,12},{... | collective-permute-start | bytes 2312 | tf_op jit(solution)/shard_map/ppermute | solution.py:21
